TPU v7x, 32 devices: a whole 2x2x4 slice. The times are simulated.
32 devices in a mesh: dp: 8 (over z, x), mp: 4 (over y, core).
Axes of the slice: x: 2, y: 2, z: 4, core: 2. Of those that a mesh axis runs over, the one named last changes fastest.
Arguments:
- acts: bfloat16 [2048, 4096], P('dp'), may hold values from -6 to 6
- cotangent: bfloat16 [2048, 2048], P('dp', 'mp'), may hold values from -0.13183594 to 0.13183594
- stats: float32 [4, 8, 2, 512, 512], P('mp', 'dp'), as said below
- owner_slot: int32 [8], replicated, may hold values from 0 to 7, as said below
Outputs:
- update: bfloat16 [8, 512, 2048], P(None, 'dp', 'mp')
- new_stats: float32 [4, 8, 2, 512, 512], P('mp', 'dp')
Inputs may be any that keep to these rules, and one draw needn't show every extreme that they name: Distinct slot numbers; row block w is held by device owner_slot[w] // 1 of dp at its position owner_slot[w] % 1; some device holds 1 block. Every stats[j, s, f] is a symmetric positive definite matrix.
All inputs are finite; a program needn't handle non-finite values.
Results may differ from a plain program's by a relative error of at most 0.012.
The roundings to bfloat16 on the way count: a program that leaves them out, or rounds other values in their place, can miss the bound.
Values may be sent and summed in bfloat16 or wider, within the bound.
A program may use at most 192 MiB of HBM per device.

v0:
```python
import jax
import jax.numpy as jnp
from jax import lax
from jax.sharding import PartitionSpec as P

ITERS = 5
BETA = 0.9
DAMPING = 0.001
EPSILON = 1e-06


def batched(former, latter):
    return jnp.einsum(
        "kij,kjl->kil",
        former.astype(jnp.bfloat16),
        latter.astype(jnp.bfloat16),
        preferred_element_type=jnp.float32,
    )


def inverse_roots(stat_pair):
    identity = jnp.eye(stat_pair.shape[-1], dtype=jnp.float32)
    damped = stat_pair + DAMPING * identity
    frob_norm = jnp.sqrt(jnp.sum(damped * damped, axis=(1, 2), keepdims=True) + EPSILON)
    moment = damped / frob_norm
    result = jnp.broadcast_to(identity, stat_pair.shape)
    for iteration in range(ITERS):
        factor = (5.0 * identity - moment) * 0.25
        if iteration == 0:
            result = factor
        else:
            result = batched(result, factor)
        if iteration + 1 < ITERS:
            square = batched(factor, factor)
            moment = batched(square, batched(square, moment))
    return result * frob_norm ** (-0.25)


def precondition(grad_block, stat_pair):
    gram_left = lax.dot_general(
        grad_block, grad_block, (((1,), (1,)), ((), ())), preferred_element_type=jnp.float32
    )
    gram_right = lax.dot_general(
        grad_block, grad_block, (((0,), (0,)), ((), ())), preferred_element_type=jnp.float32
    )
    new_pair = BETA * stat_pair + (1.0 - BETA) * jnp.stack([gram_left, gram_right])
    root_pair = inverse_roots(new_pair)
    left_applied = jnp.dot(
        root_pair[0].astype(jnp.bfloat16), grad_block, preferred_element_type=jnp.float32
    )
    direction = jnp.dot(
        left_applied.astype(jnp.bfloat16),
        root_pair[1].astype(jnp.bfloat16),
        preferred_element_type=jnp.float32,
    )
    grad_wide = grad_block.astype(jnp.float32)
    graft_ratio = jnp.sqrt(
        (jnp.mean(grad_wide * grad_wide) + EPSILON) / (jnp.mean(direction * direction) + EPSILON)
    )
    return ((direction * graft_ratio).astype(jnp.bfloat16), new_pair)


def keep_slot(grad_block, stat_pair):
    return (jnp.zeros_like(grad_block), stat_pair)


def on_device(acts, cotangent, stats, owner_slot):
    dp_count = lax.axis_size("dp")
    my_index = lax.axis_index("dp")
    blk_size = cotangent.shape[1]
    blocks = acts.shape[1] // blk_size
    slot_count = stats.shape[1]
    piece_rows = blk_size // dp_count
    split_acts = acts.reshape(acts.shape[0], blocks, blk_size)
    my_slots = my_index * slot_count + jnp.arange(slot_count, dtype=jnp.int32)
    holds_block = owner_slot[None, :] == my_slots[:, None]
    filled = jnp.any(holds_block, axis=1)
    my_rows = lax.psum_scatter(
        jnp.einsum("twr,tc->rwc", split_acts, cotangent, preferred_element_type=jnp.float32),
        "dp",
        scatter_dimension=0,
        tiled=True,
    ).astype(jnp.bfloat16)
    slot_ids = jnp.arange(dp_count * slot_count, dtype=jnp.int32)
    selector = (owner_slot[None, :] == slot_ids[:, None]).astype(jnp.bfloat16)
    outgoing = jnp.einsum(
        "sw,rwc->src", selector, my_rows, preferred_element_type=jnp.float32
    ).astype(jnp.bfloat16)
    outgoing = outgoing.reshape(dp_count, slot_count, piece_rows, blk_size)
    arrived = lax.all_to_all(outgoing, "dp", split_axis=0, concat_axis=2, tiled=True)
    owned_grads = arrived.reshape(slot_count, blk_size, blk_size)
    slot_update, slot_stats = lax.cond(
        filled[0], precondition, keep_slot, owned_grads[0], stats[0, 0]
    )
    update_list = [slot_update]
    stat_list = [slot_stats]
    updates = jnp.stack(update_list)
    new_stats = jnp.stack(stat_list)[None]
    outgoing_rows = updates.reshape(slot_count, dp_count, piece_rows, blk_size)
    returned = lax.all_to_all(outgoing_rows, "dp", split_axis=1, concat_axis=1, tiled=True)
    grid_ids = (
        jnp.arange(slot_count, dtype=jnp.int32)[:, None]
        + slot_count * jnp.arange(dp_count, dtype=jnp.int32)[None, :]
    )
    picker = (owner_slot[:, None, None] == grid_ids[None]).astype(jnp.bfloat16)
    result = jnp.einsum(
        "wsn,snrc->wrc", picker, returned, preferred_element_type=jnp.float32
    ).astype(jnp.bfloat16)
    return (result, new_stats)


def solution(mesh):
    return jax.shard_map(
        on_device,
        mesh=mesh,
        in_specs=(P("dp", None), P("dp", "mp"), P("mp", "dp", None, None, None), P()),
        out_specs=(P(None, "dp", "mp"), P("mp", "dp", None, None, None)),
        check_vma=False,
    )
```

profile of v0, /device:TPU:0, one launch (start us, length us, event | category | flops | bytes accessed | tf_op | source)
XLA Modules:
  0.0 265.3 jit_solution(8592918326225802116)
XLA Ops:
  7.2 3.2 %copy.27 = f32[1,1,2,512,512]{4,3,2,1,0:T(8,128)} copy(f32[1,1,2,512,512]{4,3,2,1,0:T(8,128)} %param.8) | data formatting | bytes 4194304
  11.4 3.5 %copy.11 = bf16[256,8,512]{0,1,2:T(8,128)(2,1)} copy(bf16[256,8,512]{2,1,0:T(8,128)(2,1)S(1)} %bitcast.62) | data formatting | bytes 4194304 | tf_op jit(solution)/shard_map/reshape | solution.py:74
  14.8 6.1 %convolution_bitcast_fusion.2 = f32[512,8,512]{2,1,0:T(8,128)} fusion(bf16[256,8,512]{0,1,2:T(8,128)(2,1)} %copy.11, bf16[256,512]{1,0:T(8,128)(2,1)S(1)} %copy-done), kind=kOutput, calls=%fused_computation.43 | convolution fusion | flops 1073741824 | bytes 10747904 | tf_op jit(solution)/shard_map/twr,tc->rwc/dot_general | solution.py:79
  20.9 150.3 %reduce-scatter.2.cloned.1.call-done = f32[64,8,512]{2,1,0:T(8,128)} async-done(((f32[512,8,512]{2,1,0:T(8,128)}), f32[64,8,512]{2,1,0:T(8,128)}) %reduce-scatter.2.cloned.1.call-update) | async-done | bytes 1048592 | tf_op jit(solution)/shard_map/reduce_scatter | solution.py:78
  171.3 1.5 fusion.16
  173.7 3.7 %all-to-all-start = ((bf16[8,1,64,512]{3,2,1,0:T(8,128)(2,1)}), bf16[8,1,64,512]{3,2,1,0:T(8,128)(2,1)S(1)}, u32[]{:S(2)}, u32[]{:S(2)}) async-start(bf16[8,1,64,512]{3,2,1,0:T(8,128)(2,1)} %copy.12), calls=%async_computation.1 | async-start | bytes 1048576 | tf_op jit(solution)/shard_map/all_to_all | solution.py:90
  178.9 13.2 %all-to-all-done = bf16[8,1,64,512]{3,2,1,0:T(8,128)(2,1)S(1)} async-done(((bf16[8,1,64,512]{3,2,1,0:T(8,128)(2,1)}), bf16[8,1,64,512]{3,2,1,0:T(8,128)(2,1)S(1)}, u32[]{:S(2)}, u32[]{:S(2)}) %all-to-all-start) | async-done | bytes 524320 | tf_op jit(solution)/shard_map/all_to_all | solution.py:90
  192.1 46.7 %conditional.1 = (bf16[512,512]{1,0:T(8,128)(2,1)}, f32[2,512,512]{2,1,0:T(8,128)}) conditional(s32[]{:T(128)} %convert_element_type.105, f32[2,512,512]{2,1,0:T(8,128)} %bitcast.65, (f32[2,512,512]{2,1,0:T(8,128)}, bf16[8,1,64,512]{3,2,1,0:T(8,128)(2,1)S(1)}) %tuple.32), branch_computations={%region_2.0_spmd, %region_3.0_spmd} | conditional | flops 9696444416 | bytes 114819456 | solution.py:92
  193.4 1.1 copy-done.5
  194.5 1.6 multiply_reduce_fusion
  196.1 1.3 copy-done.6
  197.4 2.2 convolution_convert_fusion.10
  199.6 3.8 %fusion.1 = f32[2,512,512]{2,1,0:T(8,128)S(1)} fusion(bf16[2,512,512]{2,1,0:T(8,128)(2,1)} %convolution_convert_fusion.10, f32[2,512,512]{2,1,0:T(8,128)} %copy-done.6, f32[2]{0:T(128)S(1)} %get-tuple-element.29, f32[512,512]{1,0:T(8,128)} %copy-done.7), kind=kOutput, calls=%fused_computation.21 | convolution fusion | flops 1075838976 | bytes 6291464 | tf_op jit(solution)/shard_map/cond/branch_1_fun/kij,kjl->kil/dot_general | solution.py:13
  203.4 1.3 copy-done.2
  204.8 1.7 convolution_convert_fusion.7
  206.5 3.5 %fusion.2 = f32[2,512,512]{2,1,0:T(8,128)S(1)} fusion(bf16[2,512,512]{2,1,0:T(8,128)(2,1)} %convolution_convert_fusion.7, f32[2,512,512]{2,1,0:T(8,128)} %copy-done.2), kind=kOutput, calls=%fused_computation.22 | convolution fusion | flops 1074790400 | bytes 5242880 | tf_op jit(solution)/shard_map/cond/branch_1_fun/kij,kjl->kil/dot_general | solution.py:13
  210.0 5.0 %convolution_convert_fusion.5 = bf16[2,512,512]{2,1,0:T(8,128)(2,1)} fusion(f32[512,512]{1,0:T(8,128)S(1)} %get-tuple-element.33, f32[2,512,512]{2,1,0:T(8,128)} %copy-done.2, f32[2,512,512]{2,1,0:T(8,128)S(1)} %fusion.2, f32[2,512,512]{2,1,0:T(8,128)} %copy-done.6, f32[2]{0:T(128)S(1)} %get-tuple-element.29, f32[512,512]{1,0:T(8,128)} %copy-done.7), kind=kOutput, calls=%fused_computation.15 | convolution fusion | flops 1080557568 | bytes 9437192 | tf_op jit(solution)/shard_map/cond/branch_1_fun/kij,kjl->kil/dot_general | solution.py:13
  215.0 1.7 convolution_convert_fusion.4
  216.7 4.2 %fusion.3 = f32[2,512,512]{2,1,0:T(8,128)} fusion(bf16[2,512,512]{2,1,0:T(8,128)(2,1)} %convolution_convert_fusion.4, f32[2,512,512]{2,1,0:T(8,128)S(1)} %fusion.2), kind=kOutput, calls=%fused_computation.23 | convolution fusion | flops 1074790400 | bytes 5242880 | tf_op jit(solution)/shard_map/cond/branch_1_fun/kij,kjl->kil/dot_general | solution.py:13
  220.9 4.1 %convolution_convert_fusion.1 = bf16[2,512,512]{2,1,0:T(8,128)(2,1)} fusion(f32[2,512,512]{2,1,0:T(8,128)} %fusion.3, f32[512,512]{1,0:T(8,128)S(1)} %get-tuple-element.33), kind=kOutput, calls=%fused_computation.11 | convolution fusion | flops 538968064 | bytes 4194304 | tf_op jit(solution)/shard_map/cond/branch_1_fun/kij,kjl->kil/dot_general | solution.py:13
  225.0 3.8 %multiply_convert_fusion.1 = bf16[2,512,512]{2,1,0:T(8,128)(2,1)} fusion(bf16[2,512,512]{2,1,0:T(8,128)(2,1)} %convolution_convert_fusion.1, f32[2,512,512]{2,1,0:T(8,128)S(1)} %copy-done.1, f32[512,512]{1,0:T(8,128)S(1)} %get-tuple-element.33), kind=kOutput, calls=%fused_computation.3 | convolution fusion | flops 1076363264 | bytes 5242880 | tf_op jit(solution)/shard_map/cond/branch_1_fun/kij,kjl->kil/dot_general | solution.py:13
  228.8 3.9 %multiply_convert_fusion = bf16[2,512,512]{2,1,0:T(8,128)(2,1)} fusion(bf16[2,512,512]{2,1,0:T(8,128)(2,1)} %multiply_convert_fusion.1, bf16[2,512,512]{2,1,0:T(8,128)(2,1)} %convolution_convert_fusion.5, f32[2]{0:T(128)S(1)} %get-tuple-element.28, f32[2,512,512]{2,1,0:T(8,128)S(1)} %copy-done.1, f32[512,512]{1,0:T(8,128)S(1)} %get-tuple-element.33), kind=kOutput, calls=%fused_computation.2 | convolution fusion | flops 1076887552 | bytes 6291464 | tf_op jit(solution)/shard_map/cond/branch_1_fun/kij,kjl->kil/dot_general | solution.py:13
  232.6 2.9 %multiply_reduce_fusion.1 = (f32[]{:T(128)}, f32[512,512]{1,0:T(8,128)S(1)}) fusion(bf16[2,512,512]{2,1,0:T(8,128)(2,1)} %multiply_convert_fusion, bf16[512,512]{1,0:T(8,128)(2,1)} %bitcast.64), kind=kOutput, calls=%fused_computation.29 | convolution fusion | flops 537657344 | bytes 2621444 | tf_op jit(solution)/shard_map/cond/branch_1_fun/dot_general | solution.py:51
  238.8 18.3 %all_to_all.14 = bf16[1,8,64,512]{3,2,0,1:T(8,128)(2,1)S(1)} all-to-all(bf16[1,8,64,512]{3,2,0,1:T(8,128)(2,1)} %bitcast.16), channel_id=1, replica_groups=mesh['dp'=8,'mp'=4] {'dp'}, dimensions={1} | all-to-all | bytes 1048576 | tf_op jit(solution)/shard_map/all_to_all | solution.py:100
  (30 shorter events, 7.1 us)
Async XLA Ops:
  7.2 7.7 %copy-start = (bf16[256,512]{1,0:T(8,128)(2,1)S(1)}, bf16[256,512]{1,0:T(8,128)(2,1)}, u32[]{:S(2)}) copy-start(bf16[256,512]{1,0:T(8,128)(2,1)} %param.7) | copy-start | bytes 786436
  7.2 164.1 %reduce-scatter.2.cloned.1.call-start = ((), (), s32[]{:S(2)}) async-start(), calls=%async_computation.3 | async-start | bytes 9437184 | tf_op jit(solution)/shard_map/reduce_scatter | solution.py:78
  7.2 3.2 %copy-start.8 = (bf16[256,4096]{1,0:T(8,128)(2,1)S(1)}, bf16[256,4096]{1,0:T(8,128)(2,1)}, u32[]{:S(2)}) copy-start(bf16[256,4096]{1,0:T(8,128)(2,1)} %param.6) | copy-start | bytes 6291460
  20.9 150.4 %copy-start.9 = (s32[8]{0:T(128)S(1)}, s32[8]{0:T(128)}, u32[]{:S(2)}) copy-start(s32[8]{0:T(128)} %param.9) | copy-start | bytes 100
  173.7 18.4 %all-to-all-start = ((bf16[8,1,64,512]{3,2,1,0:T(8,128)(2,1)}), bf16[8,1,64,512]{3,2,1,0:T(8,128)(2,1)S(1)}, u32[]{:S(2)}, u32[]{:S(2)}) async-start(bf16[8,1,64,512]{3,2,1,0:T(8,128)(2,1)} %copy.12), calls=%async_computation.1 | async-start | bytes 1048576 | tf_op jit(solution)/shard_map/all_to_all | solution.py:90
  192.1 0.8 copy-start.3
  192.2 3.9 %copy-start.7 = (f32[512,512]{1,0:T(8,128)}, f32[512,512]{1,0:T(8,128)S(1)}, u32[]{:S(2)}) copy-start(f32[512,512]{1,0:T(8,128)S(1)} %get-tuple-element.32) | copy-start | bytes 3145732 | tf_op jit(solution)/shard_map/cond
  192.9 1.6 copy-start.5
  196.1 1.3 copy-start.6
  203.4 1.4 copy-start.2
  220.9 4.1 %copy-start.1 = (f32[2,512,512]{2,1,0:T(8,128)S(1)}, f32[2,512,512]{2,1,0:T(8,128)}, u32[]{:S(2)}) copy-start(f32[2,512,512]{2,1,0:T(8,128)} %fusion.3) | copy-start | bytes 6291460 | tf_op jit(solution)/shard_map/cond
  232.6 3.6 %copy-start.4 = (bf16[8,1,64,512]{3,2,1,0:T(8,128)(2,1)S(1)}, bf16[8,1,64,512]{3,2,1,0:T(8,128)(2,1)}, u32[]{:S(2)}) copy-start(bf16[8,1,64,512]{3,2,1,0:T(8,128)(2,1)} %copy-done.3) | copy-start | bytes 1572868 | tf_op jit(solution)/shard_map/cond
Sparse Core Ops, SparseCore 0:
  21.1 150.1 reduce-scatter.1
where the time goes:
time: 266 us; the launch traced here: 265 us
  waiting for transfers between devices  164 us (62%)
  matrix products  45.7 us (17%)
  blocking collectives  18.3 us (7%)
  between operations  14.8 us (6%)
  local copies, waits for them, and re-layouts  13.5 us (5%)
  other arithmetic  4.26 us (2%)
  starting transfers between devices  3.75 us (1%)
    reduce_scatter x1, waiting for transfers between devices, on_device(): lax.psum_scatter(jnp.einsum('twr,tc->rwc', split_acts, cotangent, preferr...  150 us
    dot_general x10, matrix products, batched(): jnp.einsum('kij,kjl->kil', former.astype(jnp.bfloat16), latter.astype(jnp...  33.9 us
    all_to_all x1, blocking collectives, on_device(): lax.all_to_all(outgoing_rows, 'dp', split_axis=1, concat_axis=1, tiled=True)  18.3 us
    all_to_all x1, waiting for transfers between devices, on_device(): lax.all_to_all(outgoing, 'dp', split_axis=0, concat_axis=2, tiled=True)  13.2 us
    dot_general x1, matrix products, on_device(): jnp.einsum('twr,tc->rwc', split_acts, cotangent, preferred_element_type=j...  6.07 us
  transfers between devices with their start and end apart: 2, of which 2 were waited for; matrix products, arithmetic and copies ran while one was open for 0% of the time, Pallas kernels for 0%

commit v1 on v0

--- a/solution.py
+++ b/solution.py
@@ -87,7 +87,11 @@
         "sw,rwc->src", selector, my_rows, preferred_element_type=jnp.float32
     ).astype(jnp.bfloat16)
     outgoing = outgoing.reshape(dp_count, slot_count, piece_rows, blk_size)
-    arrived = lax.all_to_all(outgoing, "dp", split_axis=0, concat_axis=2, tiled=True)
+    _start_sheets = lambda tile_in: jnp.concatenate(
+        lax.all_to_all(jnp.stack(jnp.split(tile_in, lax.axis_size("dp"), axis=0)), "dp", 0, 0),
+        axis=2,
+    )
+    arrived = _start_sheets(outgoing)
     owned_grads = arrived.reshape(slot_count, blk_size, blk_size)
     slot_update, slot_stats = lax.cond(
         filled[0], precondition, keep_slot, owned_grads[0], stats[0, 0]

time: 266 us -> 271 us (1.019)
  local copies, waits for them, and re-layouts: 13.5 us -> 18.6 us
    unnamed x9 -> x16, local copies, waits for them, and re-layouts: 5.09 us -> 9.57 us
where the time goes in v1:
time: 271 us; the launch traced here: 270 us
  waiting for transfers between devices  164 us (61%)
  matrix products  45.6 us (17%)
  local copies, waits for them, and re-layouts  18.6 us (7%)
  blocking collectives  18.3 us (7%)
  between operations  14.6 us (5%)
  other arithmetic  4.17 us (2%)
  starting transfers between devices  3.76 us (1%)
    reduce_scatter x1, waiting for transfers between devices, on_device(): lax.psum_scatter(jnp.einsum('twr,tc->rwc', split_acts, cotangent, preferr...  150 us
    dot_general x10, matrix products, batched(): jnp.einsum('kij,kjl->kil', former.astype(jnp.bfloat16), latter.astype(jnp...  33.8 us
    all_to_all x1, blocking collectives, on_device(): lax.all_to_all(outgoing_rows, 'dp', split_axis=1, concat_axis=1, tiled=True)  18.3 us
    all_to_all x1, waiting for transfers between devices, on_device(): lax.all_to_all(jnp.stack(jnp.split(tile_in, lax.axis_size('dp'), axis=0))...  13.4 us
    unnamed x16, local copies, waits for them, and re-layouts  9.57 us
    dot_general x1, matrix products, on_device(): jnp.einsum('twr,tc->rwc', split_acts, cotangent, preferred_element_type=j...  6.08 us
  transfers between devices with their start and end apart: 2, of which 2 were waited for; matrix products, arithmetic and copies ran while one was open for 0% of the time, Pallas kernels for 0%

profile of v1, /device:TPU:0, one launch (start us, length us, event | category | flops | bytes accessed | tf_op | source)
XLA Modules:
  0.0 270.2 jit_solution(17714748441440273184)
XLA Ops:
  7.2 3.2 %copy.105 = f32[1,1,2,512,512]{4,3,2,1,0:T(8,128)} copy(f32[1,1,2,512,512]{4,3,2,1,0:T(8,128)} %param.8) | data formatting | bytes 4194304
  11.4 3.5 %copy.67 = bf16[256,8,512]{0,1,2:T(8,128)(2,1)} copy(bf16[256,8,512]{2,1,0:T(8,128)(2,1)S(1)} %bitcast.77) | data formatting | bytes 4194304 | tf_op jit(solution)/shard_map/reshape | solution.py:74
  14.8 6.1 %convolution_bitcast_fusion.2 = f32[512,8,512]{2,1,0:T(8,128)} fusion(bf16[256,8,512]{0,1,2:T(8,128)(2,1)} %copy.67, bf16[256,512]{1,0:T(8,128)(2,1)S(1)} %copy-done), kind=kOutput, calls=%fused_computation.43 | convolution fusion | flops 1073741824 | bytes 10747904 | tf_op jit(solution)/shard_map/twr,tc->rwc/dot_general | solution.py:79
  20.9 150.3 %reduce-scatter.2.cloned.1.call-done = f32[64,8,512]{2,1,0:T(8,128)} async-done(((f32[512,8,512]{2,1,0:T(8,128)}), f32[64,8,512]{2,1,0:T(8,128)}) %reduce-scatter.2.cloned.1.call-update) | async-done | bytes 1048592 | tf_op jit(solution)/shard_map/reduce_scatter | solution.py:78
  171.3 1.5 convolution_convert_fusion.13
  178.9 3.7 %all-to-all-start = ((bf16[8,1,1,64,512]{4,3,2,1,0:T(8,128)(2,1)}), bf16[8,1,1,64,512]{4,3,2,1,0:T(8,128)(2,1)S(1)}, u32[]{:S(2)}, u32[]{:S(2)}) async-start(bf16[8,1,1,64,512]{4,3,2,1,0:T(8,128)(2,1)} %bitcast_dynamic-update-slice_fusion), calls=%async_computation.1 | async-start | bytes 1048576 | tf_op jit(solution)/shard_map/all_to_all | solution.py:91
  183.8 13.4 %all-to-all-done = bf16[8,1,1,64,512]{4,3,2,1,0:T(8,128)(2,1)S(1)} async-done(((bf16[8,1,1,64,512]{4,3,2,1,0:T(8,128)(2,1)}), bf16[8,1,1,64,512]{4,3,2,1,0:T(8,128)(2,1)S(1)}, u32[]{:S(2)}, u32[]{:S(2)}) %all-to-all-start) | async-done | bytes 524320 | tf_op jit(solution)/shard_map/all_to_all | solution.py:91
  197.2 46.4 %conditional.1 = (bf16[512,512]{1,0:T(8,128)(2,1)}, f32[2,512,512]{2,1,0:T(8,128)}) conditional(s32[]{:T(128)} %convert_element_type.105, f32[2,512,512]{2,1,0:T(8,128)} %bitcast.80, (f32[2,512,512]{2,1,0:T(8,128)}, bf16[8,1,1,64,512]{4,3,2,1,0:T(8,128)(2,1)S(1)}) %tuple.53), branch_computations={%region_2.0_spmd, %region_3.0_spmd} | conditional | flops 9696444416 | bytes 114819456 | solution.py:96
  198.5 1.1 copy-done.5
  199.6 1.6 multiply_reduce_fusion
  201.3 1.3 copy-done.6
  202.5 2.2 convolution_convert_fusion.10
  204.7 3.8 %fusion.1 = f32[2,512,512]{2,1,0:T(8,128)S(1)} fusion(bf16[2,512,512]{2,1,0:T(8,128)(2,1)} %convolution_convert_fusion.10, f32[2,512,512]{2,1,0:T(8,128)} %copy-done.6, f32[2]{0:T(128)S(1)} %get-tuple-element.57, f32[512,512]{1,0:T(8,128)} %copy-done.7), kind=kOutput, calls=%fused_computation.21 | convolution fusion | flops 1075838976 | bytes 6291464 | tf_op jit(solution)/shard_map/cond/branch_1_fun/kij,kjl->kil/dot_general | solution.py:13
  208.6 1.3 copy-done.2
  209.9 1.7 convolution_convert_fusion.7
  211.6 3.5 %fusion.2 = f32[2,512,512]{2,1,0:T(8,128)S(1)} fusion(bf16[2,512,512]{2,1,0:T(8,128)(2,1)} %convolution_convert_fusion.7, f32[2,512,512]{2,1,0:T(8,128)} %copy-done.2), kind=kOutput, calls=%fused_computation.22 | convolution fusion | flops 1074790400 | bytes 5242880 | tf_op jit(solution)/shard_map/cond/branch_1_fun/kij,kjl->kil/dot_general | solution.py:13
  215.1 5.0 %convolution_convert_fusion.5 = bf16[2,512,512]{2,1,0:T(8,128)(2,1)} fusion(f32[512,512]{1,0:T(8,128)S(1)} %get-tuple-element.61, f32[2,512,512]{2,1,0:T(8,128)} %copy-done.2, f32[2,512,512]{2,1,0:T(8,128)S(1)} %fusion.2, f32[2,512,512]{2,1,0:T(8,128)} %copy-done.6, f32[2]{0:T(128)S(1)} %get-tuple-element.57, f32[512,512]{1,0:T(8,128)} %copy-done.7), kind=kOutput, calls=%fused_computation.15 | convolution fusion | flops 1080557568 | bytes 9437192 | tf_op jit(solution)/shard_map/cond/branch_1_fun/kij,kjl->kil/dot_general | solution.py:13
  220.1 1.7 convolution_convert_fusion.4
  221.8 4.1 %fusion.3 = f32[2,512,512]{2,1,0:T(8,128)} fusion(bf16[2,512,512]{2,1,0:T(8,128)(2,1)} %convolution_convert_fusion.4, f32[2,512,512]{2,1,0:T(8,128)S(1)} %fusion.2), kind=kOutput, calls=%fused_computation.23 | convolution fusion | flops 1074790400 | bytes 5242880 | tf_op jit(solution)/shard_map/cond/branch_1_fun/kij,kjl->kil/dot_general | solution.py:13
  226.0 4.1 %convolution_convert_fusion.1 = bf16[2,512,512]{2,1,0:T(8,128)(2,1)} fusion(f32[2,512,512]{2,1,0:T(8,128)} %fusion.3, f32[512,512]{1,0:T(8,128)S(1)} %get-tuple-element.61), kind=kOutput, calls=%fused_computation.11 | convolution fusion | flops 538968064 | bytes 4194304 | tf_op jit(solution)/shard_map/cond/branch_1_fun/kij,kjl->kil/dot_general | solution.py:13
  230.1 3.8 %multiply_convert_fusion.1 = bf16[2,512,512]{2,1,0:T(8,128)(2,1)} fusion(bf16[2,512,512]{2,1,0:T(8,128)(2,1)} %convolution_convert_fusion.1, f32[2,512,512]{2,1,0:T(8,128)S(1)} %copy-done.1, f32[512,512]{1,0:T(8,128)S(1)} %get-tuple-element.61), kind=kOutput, calls=%fused_computation.3 | convolution fusion | flops 1076363264 | bytes 5242880 | tf_op jit(solution)/shard_map/cond/branch_1_fun/kij,kjl->kil/dot_general | solution.py:13
  233.8 3.9 %multiply_convert_fusion = bf16[2,512,512]{2,1,0:T(8,128)(2,1)} fusion(bf16[2,512,512]{2,1,0:T(8,128)(2,1)} %multiply_convert_fusion.1, bf16[2,512,512]{2,1,0:T(8,128)(2,1)} %convolution_convert_fusion.5, f32[2]{0:T(128)S(1)} %get-tuple-element.56, f32[2,512,512]{2,1,0:T(8,128)S(1)} %copy-done.1, f32[512,512]{1,0:T(8,128)S(1)} %get-tuple-element.61), kind=kOutput, calls=%fused_computation.2 | convolution fusion | flops 1076887552 | bytes 6291464 | tf_op jit(solution)/shard_map/cond/branch_1_fun/kij,kjl->kil/dot_general | solution.py:13
  237.7 2.9 %multiply_reduce_fusion.1 = (f32[]{:T(128)}, f32[512,512]{1,0:T(8,128)S(1)}) fusion(bf16[2,512,512]{2,1,0:T(8,128)(2,1)} %multiply_convert_fusion, bf16[512,512]{1,0:T(8,128)(2,1)} %bitcast.79), kind=kOutput, calls=%fused_computation.29 | convolution fusion | flops 537657344 | bytes 2621444 | tf_op jit(solution)/shard_map/cond/branch_1_fun/dot_general | solution.py:51
  243.6 18.3 %all_to_all.10 = bf16[1,8,64,512]{3,2,0,1:T(8,128)(2,1)S(1)} all-to-all(bf16[1,8,64,512]{3,2,0,1:T(8,128)(2,1)} %bitcast.15), channel_id=1, replica_groups=mesh['dp'=8,'mp'=4] {'dp'}, dimensions={1} | all-to-all | bytes 1048576 | tf_op jit(solution)/shard_map/all_to_all | solution.py:104
  (38 shorter events, 12.1 us)
Async XLA Ops:
  7.2 7.7 %copy-start = (bf16[256,512]{1,0:T(8,128)(2,1)S(1)}, bf16[256,512]{1,0:T(8,128)(2,1)}, u32[]{:S(2)}) copy-start(bf16[256,512]{1,0:T(8,128)(2,1)} %param.7) | copy-start | bytes 786436
  7.2 164.1 %reduce-scatter.2.cloned.1.call-start = ((), (), s32[]{:S(2)}) async-start(), calls=%async_computation.3 | async-start | bytes 9437184 | tf_op jit(solution)/shard_map/reduce_scatter | solution.py:78
  7.2 3.2 %copy-start.8 = (bf16[256,4096]{1,0:T(8,128)(2,1)S(1)}, bf16[256,4096]{1,0:T(8,128)(2,1)}, u32[]{:S(2)}) copy-start(bf16[256,4096]{1,0:T(8,128)(2,1)} %param.6) | copy-start | bytes 6291460
  20.9 150.4 %copy-start.9 = (s32[8]{0:T(128)S(1)}, s32[8]{0:T(128)}, u32[]{:S(2)}) copy-start(s32[8]{0:T(128)} %param.9) | copy-start | bytes 100
  178.9 18.3 %all-to-all-start = ((bf16[8,1,1,64,512]{4,3,2,1,0:T(8,128)(2,1)}), bf16[8,1,1,64,512]{4,3,2,1,0:T(8,128)(2,1)S(1)}, u32[]{:S(2)}, u32[]{:S(2)}) async-start(bf16[8,1,1,64,512]{4,3,2,1,0:T(8,128)(2,1)} %bitcast_dynamic-update-slice_fusion), calls=%async_computation.1 | async-start | bytes 1048576 | tf_op jit(solution)/shard_map/all_to_all | solution.py:91
  197.2 0.8 copy-start.3
  197.4 3.9 %copy-start.7 = (f32[512,512]{1,0:T(8,128)}, f32[512,512]{1,0:T(8,128)S(1)}, u32[]{:S(2)}) copy-start(f32[512,512]{1,0:T(8,128)S(1)} %get-tuple-element.60) | copy-start | bytes 3145732 | tf_op jit(solution)/shard_map/cond
  198.0 1.6 copy-start.5
  201.2 1.3 copy-start.6
  208.5 1.3 copy-start.2
  226.0 4.1 %copy-start.1 = (f32[2,512,512]{2,1,0:T(8,128)S(1)}, f32[2,512,512]{2,1,0:T(8,128)}, u32[]{:S(2)}) copy-start(f32[2,512,512]{2,1,0:T(8,128)} %fusion.3) | copy-start | bytes 6291460 | tf_op jit(solution)/shard_map/cond
  237.7 3.4 %copy-start.4 = (bf16[8,1,1,64,512]{4,3,2,1,0:T(8,128)(2,1)S(1)}, bf16[8,1,1,64,512]{4,3,2,1,0:T(8,128)(2,1)}, u32[]{:S(2)}) copy-start(bf16[8,1,1,64,512]{4,3,2,1,0:T(8,128)(2,1)} %copy-done.3) | copy-start | bytes 1572868 | tf_op jit(solution)/shard_map/cond
Sparse Core Ops, SparseCore 0:
  21.1 150.1 reduce-scatter.1
